TPU v7x, 32 devices: a whole 2x2x4 slice. The times are simulated.
32 devices in a mesh: expert: 4 (over x, core), replica: 8 (over z, y).
Axes of the slice: x: 2, y: 2, z: 4, core: 2. Of those that a mesh axis runs over, the one named last changes fastest.
Arguments:
- tokens: bfloat16 [192, 4096], P(('expert', 'replica')), may hold values from -6 to 6
- out_grad: bfloat16 [192, 4096], P(('expert', 'replica')), may hold values from -2.5 to 2.5
- expert_ids: int32 [192, 2], P(('expert', 'replica')), may hold values from 0 to 3, all different within a row; in each aligned block of 6 rows (0 to 5, 6 to 11, ...) at most 4 rows name the same one
- gates: float32 [192, 2], P(('expert', 'replica')), may hold values from 0.1 to 1
- w_gate: bfloat16 [4, 7168, 4096], P('expert', 'replica'), may hold values from -0.09375 to 0.09375
- w_up: bfloat16 [4, 7168, 4096], P('expert', 'replica'), may hold values from -0.09375 to 0.09375
- w_down: bfloat16 [4, 7168, 4096], P('expert', 'replica'), may hold values from -0.0625 to 0.0625
Outputs:
- gate_grad: float32 [192, 2], P(('expert', 'replica'))
- input_grad: bfloat16 [192, 4096], P(('expert', 'replica'))
- grad_gate: bfloat16 [4, 7168, 4096], P('expert', 'replica')
- grad_up: bfloat16 [4, 7168, 4096], P('expert', 'replica')
- grad_down: bfloat16 [4, 7168, 4096], P('expert', 'replica')
Inputs may be any that keep to these rules, and one draw needn't show every extreme that they name: `expert_ids`: each row names 2 different experts; among the rows of one device no expert is named more than 4 times.
All inputs are finite; a program needn't handle non-finite values.
Results may differ from a plain program's by a relative error of at most 0.02.
Values may be sent and summed in bfloat16 or wider, within the bound.
A program may use at most 128 MiB of HBM per device.

v0:
```python
import jax
import jax.numpy as jnp
from jax import lax
from jax.sharding import PartitionSpec as P


def on_device(tokens, out_grad, expert_ids, gates, w_gate, w_up, w_down):
    token_count = tokens.shape[0]
    fan_out = expert_ids.shape[1]
    model_width = tokens.shape[1]
    owners = lax.axis_size("expert")
    capacity = max(2, 4 * token_count * fan_out // (3 * owners))
    slot_count = owners * capacity
    flat_ids = expert_ids.reshape(-1)
    sequence_pos = jnp.arange(token_count * fan_out, dtype=jnp.int32)
    earlier = sequence_pos[None, :] < sequence_pos[:, None]
    same_expert = flat_ids[:, None] == flat_ids[None, :]
    slot_rank = jnp.sum(jnp.logical_and(same_expert, earlier), axis=1)
    target = flat_ids * capacity + slot_rank
    token_hot = (target[:, None] == jnp.arange(slot_count, dtype=jnp.int32)[None, :]).astype(
        jnp.float32
    )
    token_hot = token_hot.reshape(token_count, fan_out, slot_count)
    dispatch = jnp.sum(token_hot, axis=1).astype(jnp.bfloat16)
    slot_gate = jnp.sum(token_hot * gates[:, :, None], axis=(0, 1)).reshape(owners, capacity)
    leading = (((0,), (0,)), ((), ()))
    contract = (((1,), (1,)), ((), ()))
    send_inputs = (
        lax.dot_general(dispatch, tokens, leading, preferred_element_type=jnp.float32)
        .astype(jnp.bfloat16)
        .reshape(owners, capacity, model_width)
    )
    send_grads = (
        lax.dot_general(dispatch, out_grad, leading, preferred_element_type=jnp.float32)
        .astype(jnp.bfloat16)
        .reshape(owners, capacity, model_width)
    )
    gate_weight = w_gate[0]
    up_weight = w_up[0]
    down_weight = w_down[0]
    owned_inputs = lax.all_to_all(send_inputs, "expert", split_axis=0, concat_axis=0, tiled=True)
    column_inputs = lax.all_gather(owned_inputs, "replica", axis=0, tiled=True)
    gathered = column_inputs.reshape(-1, model_width)
    gate_pre = lax.dot_general(gathered, gate_weight, contract, preferred_element_type=jnp.float32)
    up_pre = lax.dot_general(gathered, up_weight, contract, preferred_element_type=jnp.float32)
    sigmoid_gate = jax.nn.sigmoid(gate_pre)
    active = gate_pre * sigmoid_gate
    hidden = (active * up_pre).astype(jnp.bfloat16)
    owned_grads = (
        lax.all_to_all(send_grads, "expert", split_axis=0, concat_axis=0, tiled=True),
        lax.all_to_all(
            slot_gate.astype(jnp.bfloat16), "expert", split_axis=0, concat_axis=0, tiled=True
        ).astype(slot_gate.dtype),
    )
    column_grads, column_gates = (
        lax.all_gather(owned_grads[0], "replica", axis=0, tiled=True),
        lax.all_gather(owned_grads[1].astype(jnp.bfloat16), "replica", axis=0, tiled=True).astype(
            jnp.float32
        ),
    )
    gathered_grad = column_grads.reshape(-1, model_width)
    row_gates = column_gates.reshape(-1)
    full_out = jnp.dot(hidden, down_weight, preferred_element_type=jnp.float32)
    partial_value = jnp.sum(gathered_grad * full_out, axis=1)
    summed_products = lax.psum_scatter(partial_value, "replica", scatter_dimension=0, tiled=True)
    returned = lax.all_to_all(
        summed_products.reshape(owners, capacity), "expert", split_axis=0, concat_axis=0, tiled=True
    )
    gate_grad = jnp.sum(token_hot * returned.reshape(-1)[None, None, :], axis=2)
    scaled = (row_gates[:, None] * gathered_grad).astype(jnp.bfloat16)
    hidden_grad = lax.dot_general(scaled, down_weight, contract, preferred_element_type=jnp.float32)
    gate_pre_grad = (
        hidden_grad * up_pre * sigmoid_gate * (1.0 + gate_pre * (1.0 - sigmoid_gate))
    ).astype(jnp.bfloat16)
    up_pre_grad = (hidden_grad * active).astype(jnp.bfloat16)
    grad_down = lax.dot_general(hidden, scaled, leading, preferred_element_type=jnp.float32).astype(
        jnp.bfloat16
    )
    grad_gate = lax.dot_general(
        gate_pre_grad, gathered, leading, preferred_element_type=jnp.float32
    ).astype(jnp.bfloat16)
    grad_up = lax.dot_general(
        up_pre_grad, gathered, leading, preferred_element_type=jnp.float32
    ).astype(jnp.bfloat16)
    slot_grad = lax.psum_scatter(
        (
            jnp.dot(gate_pre_grad, gate_weight, preferred_element_type=jnp.float32)
            + jnp.dot(up_pre_grad, up_weight, preferred_element_type=jnp.float32)
        ).astype(jnp.bfloat16),
        "replica",
        scatter_dimension=0,
        tiled=True,
    )
    slot_back = lax.all_to_all(
        slot_grad.reshape(owners, capacity, model_width),
        "expert",
        split_axis=0,
        concat_axis=0,
        tiled=True,
    )
    slot_back = slot_back.reshape(slot_count, model_width)
    input_grad = jnp.dot(dispatch, slot_back, preferred_element_type=jnp.float32).astype(
        jnp.bfloat16
    )
    return (gate_grad, input_grad, grad_gate[None], grad_up[None], grad_down[None])


def solution(mesh):
    placed = (
        P(("expert", "replica"), None),
        P(("expert", "replica"), None),
        P(("expert", "replica"), None),
        P(("expert", "replica"), None),
        P("expert", "replica", None),
        P("expert", "replica", None),
        P("expert", "replica", None),
    )
    return jax.shard_map(
        on_device,
        mesh=mesh,
        in_specs=placed,
        out_specs=(
            P(("expert", "replica"), None),
            P(("expert", "replica"), None),
            P("expert", "replica", None),
            P("expert", "replica", None),
            P("expert", "replica", None),
        ),
        check_vma=False,
    )
```

profile of v0, /device:TPU:0, one launch (start us, length us, event | category | flops | bytes accessed | tf_op | source)
XLA Modules:
  0.0 261.9 jit_solution(12565111648828209560)
XLA Ops:
  7.2 0.0 copy-start
  7.2 0.0 all-gather.6.cloned.1.call-start
  7.2 0.8 copy.29
  8.0 0.1 eq.29
  8.1 0.2 convert_reduce_fusion
  8.3 0.1 reduce_sum.48
  8.3 0.1 convert_reduce_fusion.1
  8.4 0.0 copy-done
  8.5 0.2 convolution_convert_fusion
  8.7 0.1 reshape.77
  8.8 8.7 %all_to_all.33 = bf16[4,4,4096]{2,1,0:T(4,128)(2,1)} all-to-all(bf16[4,4,4096]{2,1,0:T(4,128)(2,1)S(1)} %reshape.77), channel_id=1, replica_groups=mesh['expert'=4,'replica'=8] {'expert'}, dimensions={0} | all-to-all | bytes 262144 | tf_op jit(solution)/shard_map/all_to_all | solution.py:41
  17.5 0.0 all-gather.6.cloned.1.call-update
  17.5 0.0 all-gather.4.cloned.1.call-start
  17.6 1.1 convolution_convert_fusion.1
  18.6 0.1 reshape.76
  18.7 7.6 %all_to_all.34 = bf16[4,4,4096]{2,1,0:T(4,128)(2,1)} all-to-all(bf16[4,4,4096]{2,1,0:T(4,128)(2,1)S(1)} %reshape.76), channel_id=1, replica_groups=mesh['expert'=4,'replica'=8] {'expert'}, dimensions={0} | all-to-all | bytes 262144 | tf_op jit(solution)/shard_map/all_to_all | solution.py:50
  26.3 0.0 all-gather.4.cloned.1.call-update
  26.4 0.0 reduce-scatter.2.cloned.1.call-start
  26.4 0.8 copy.32
  27.2 1.2 dynamic-slice
  29.1 29.6 %all-gather.6.cloned.1.call-done = bf16[32,4,4096]{2,1,0:T(4,128)(2,1)} async-done(((bf16[4,4,4096]{2,1,0:T(4,128)(2,1)}), bf16[32,4,4096]{2,1,0:T(4,128)(2,1)}) %all-gather.6.cloned.1.call-update) | async-done | bytes 1048592 | tf_op jit(solution)/shard_map/all_gather | solution.py:42
  58.7 1.3 reshape.78
  60.1 0.0 copy-start.1
  60.1 5.7 %fusion.10 = f32[128,896]{1,0:T(8,128)S(1)} fusion(bf16[128,4096]{1,0:T(8,128)(2,1)S(1)} %reshape.78, bf16[1,896,4096]{2,1,0:T(8,128)(2,1)} %param.11), kind=kOutput, calls=%fused_computation.10 | convolution fusion | flops 939524096 | bytes 8847360 | tf_op jit(solution)/shard_map/dot_general | solution.py:44
  65.7 0.0 copy-done.1
  65.8 0.0 copy-start.5
  65.8 3.2 %multiply_convert_fusion.5 = (bf16[128,896]{1,0:T(8,128)(2,1)S(1)}, f32[128,896]{1,0:T(8,128)}) fusion(f32[128,896]{1,0:T(8,128)S(1)} %fusion.10, bf16[128,4096]{1,0:T(8,128)(2,1)S(1)} %reshape.78, bf16[1,896,4096]{2,1,0:T(8,128)(2,1)S(1)} %copy-done.1), kind=kOutput, calls=%fused_computation.27 | convolution fusion | flops 940212224 | bytes 9535488 | tf_op jit(solution)/shard_map/dot_general | solution.py:45
  69.0 0.0 copy-done.5
  69.0 31.0 %all-gather.4.cloned.1.call-done = bf16[32,4,4096]{2,1,0:T(4,128)(2,1)} async-done(((bf16[4,4,4096]{2,1,0:T(4,128)(2,1)}), bf16[32,4,4096]{2,1,0:T(4,128)(2,1)}) %all-gather.4.cloned.1.call-update) | async-done | bytes 1048592 | tf_op jit(solution)/shard_map/all_gather | solution.py:56
  100.0 1.3 reshape.81
  101.3 4.4 %fusion.21 = f32[128]{0:T(128)S(1)} fusion(f32[128,4096]{1,0:T(8,128)S(1)} %reshape.81, bf16[128,896]{1,0:T(8,128)(2,1)S(1)} %get-tuple-element.14, bf16[1,896,4096]{2,1,0:T(8,128)(2,1)} %param.13), kind=kOutput, calls=%fused_computation.23 | convolution fusion | flops 940572544 | bytes 9667072 | tf_op jit(solution)/shard_map/dot_general | solution.py:63
  105.7 19.2 %all-reduce = f32[128]{0:T(128)S(1)} all-reduce(f32[128]{0:T(128)S(1)} %fusion.21), channel_id=3, replica_groups=mesh['expert'=4,'replica'=8] {'replica'}, use_global_device_ids=true, to_apply=%region_3.0.clone | all-reduce | flops 128 | bytes 1024
  124.9 0.1 dynamic-slice.1
  125.0 0.1 all_to_all.23
  125.1 6.3 %all_to_all.35 = f32[4,1,4]{2,1,0:T(1,128)S(1)} all-to-all(f32[4,1,4]{2,1,0:T(1,128)S(1)} %bitcast.56), channel_id=1, replica_groups=mesh['expert'=4,'replica'=8] {'expert'}, dimensions={0} | all-to-all | bytes 128 | tf_op jit(solution)/shard_map/all_to_all | solution.py:66
  131.4 0.5 broadcast.41
  131.9 0.7 reduce.7
  132.5 0.1 mul.68
  132.6 0.2 select_reduce_fusion
  132.8 0.1 convert_element_type.100
  132.9 6.1 %all_to_all.36 = bf16[4,1,4]{2,1,0:T(2,128)(2,1)S(1)} all-to-all(bf16[4,1,4]{2,1,0:T(2,128)(2,1)S(1)} %convert_element_type.100), channel_id=1, replica_groups=mesh['expert'=4,'replica'=8] {'expert'}, dimensions={0} | all-to-all | bytes 64 | tf_op jit(solution)/shard_map/all_to_all | solution.py:51
  139.0 26.3 %all-gather = bf16[32,1,4]{2,1,0:T(2,128)(2,1)S(1)} all-gather(bf16[4,1,4]{2,1,0:T(2,128)(2,1)S(1)} %all_to_all.36), channel_id=2, replica_groups=mesh['expert'=4,'replica'=8] {'replica'}, dimensions={0}, use_global_device_ids=true | all-gather | bytes 288 | tf_op jit(solution)/shard_map/all_gather | solution.py:57
  165.3 2.9 %multiply_convert_fusion.1 = bf16[32,4,4096]{2,1,0:T(4,128)(2,1)} fusion(f32[32,4]{1,0:T(8,128)S(1)} %bitcast.55, bf16[32,4,4096]{2,1,0:T(4,128)(2,1)} %all-gather.4.cloned.1.call-done), kind=kLoop, calls=%fused_computation.22 | loop fusion | flops 1572864 | bytes 2097664 | tf_op jit(solution)/shard_map/convert_element_type | solution.py:70
  168.2 2.1 convert_element_type.89
  170.3 6.2 %multiply_convert_fusion.4 = (bf16[128,896]{1,0:T(8,128)(2,1)S(1)}, bf16[128,896]{1,0:T(8,128)(2,1)S(1)}) fusion(f32[128,896]{1,0:T(8,128)} %copy-done.5, f32[128,896]{1,0:T(8,128)} %get-tuple-element.15, bf16[128,4096]{1,0:T(8,128)(2,1)} %convert_element_type.89, bf16[1,896,4096]{2,1,0:T(8,128)(2,1)} %param.13), kind=kOutput, calls=%fused_computation.26 | convolution fusion | flops 941015040 | bytes 9764864 | tf_op jit(solution)/shard_map/dot_general | solution.py:71
  176.5 0.0 copy-start.2
  176.5 0.0 slice-start.1
  176.5 4.5 %fusion.4 = f32[128,4096]{1,0:T(8,128)S(1)} fusion(bf16[128,896]{1,0:T(8,128)(2,1)S(1)} %get-tuple-element.13, bf16[1,896,4096]{2,1,0:T(8,128)(2,1)} %param.12), kind=kOutput, calls=%fused_computation.4 | convolution fusion | flops 939524096 | bytes 9666560 | tf_op jit(solution)/shard_map/dot_general | solution.py:88
  181.0 0.0 copy-done.2
  181.0 0.0 slice-done
  181.0 0.0 slice-done.1
  181.1 2.3 fusion.18
  183.3 0.0 reduce-scatter.2.cloned.1.call-update
  183.4 0.6 copy.36
  184.0 0.1 convert_reduce_fusion.2
  184.1 0.1 mul.80
  184.2 6.1 %convert_bitcast_fusion.2 = bf16[1,896,4096]{2,1,0:T(8,128)(2,1)} fusion(bf16[128,896]{1,0:T(8,128)(2,1)} %copy-done.2, bf16[128,4096]{1,0:T(8,128)(2,1)S(1)} %reshape.78), kind=kOutput, calls=%fused_computation.14 | convolution fusion | flops 943194112 | bytes 8617984 | tf_op jit(solution)/shard_map/dot_general | solution.py:79
  190.3 5.2 %convert_bitcast_fusion = bf16[1,896,4096]{2,1,0:T(8,128)(2,1)} fusion(bf16[128,896]{1,0:T(8,128)(2,1)S(1)} %copy-done.4, f32[128,4096]{1,0:T(8,128)S(1)} %reshape.81, f32[128]{0:T(128)S(1)} %mul.80), kind=kOutput, calls=%fused_computation.12 | convolution fusion | flops 944242688 | bytes 9667072 | tf_op jit(solution)/shard_map/dot_general | solution.py:76
  195.5 49.0 %reduce-scatter.2.cloned.1.call-done = bf16[16,4096]{1,0:T(8,128)(2,1)} async-done(((bf16[128,4096]{1,0:T(8,128)(2,1)}), bf16[16,4096]{1,0:T(8,128)(2,1)}) %reduce-scatter.2.cloned.1.call-update) | async-done | bytes 131088 | tf_op jit(solution)/shard_map/reduce_scatter | solution.py:85
  244.4 1.6 reshape.79
  246.1 3.3 %all-to-all-start.4 = ((bf16[4,4,4096]{2,1,0:T(4,128)(2,1)}), bf16[4,4,4096]{2,1,0:T(4,128)(2,1)S(1)}, u32[]{:S(2)}, u32[]{:S(2)}) async-start(bf16[4,4,4096]{2,1,0:T(4,128)(2,1)} %reshape.79), calls=%async_computation.5 | async-start | bytes 262144 | tf_op jit(solution)/shard_map/all_to_all | solution.py:94
  249.4 5.1 %convert_bitcast_fusion.1 = bf16[1,896,4096]{2,1,0:T(8,128)(2,1)} fusion(bf16[128,896]{1,0:T(8,128)(2,1)S(1)} %get-tuple-element.13, bf16[128,4096]{1,0:T(8,128)(2,1)S(1)} %reshape.78), kind=kOutput, calls=%fused_computation.13 | convolution fusion | flops 943194112 | bytes 8617984 | tf_op jit(solution)/shard_map/dot_general | solution.py:82
  254.5 0.0 all-to-all-done.4
  254.6 0.8 convolution_convert_fusion.2
  (9 shorter events, 0.1 us)
Async XLA Ops:
  7.2 1.3 copy-start
  7.2 51.5 %all-gather.6.cloned.1.call-start = ((), (), s32[]{:S(2)}) async-start(), calls=%async_computation.7 | async-start | bytes 1179648 | tf_op jit(solution)/shard_map/all_gather | solution.py:42
  17.5 82.5 %all-gather.4.cloned.1.call-start = ((), (), s32[]{:S(2)}) async-start(), calls=%async_computation.6 | async-start | bytes 1179648 | tf_op jit(solution)/shard_map/all_gather | solution.py:56
  26.4 218.1 %reduce-scatter.2.cloned.1.call-start = ((), (), s32[]{:S(2)}) async-start(), calls=%async_computation.8 | async-start | bytes 1179648 | tf_op jit(solution)/shard_map/reduce_scatter | solution.py:85
  60.1 5.7 %copy-start.1 = (bf16[1,896,4096]{2,1,0:T(8,128)(2,1)S(1)}, bf16[1,896,4096]{2,1,0:T(8,128)(2,1)}, u32[]{:S(2)}) copy-start(bf16[1,896,4096]{2,1,0:T(8,128)(2,1)} %param.12) | copy-start | bytes 22020100
  65.8 3.3 %copy-start.5 = (f32[128,896]{1,0:T(8,128)}, f32[128,896]{1,0:T(8,128)S(1)}, u32[]{:S(2)}) copy-start(f32[128,896]{1,0:T(8,128)S(1)} %fusion.10) | copy-start | bytes 1376260
  69.0 36.7 %copy-start.3 = (bf16[128,896]{1,0:T(8,128)(2,1)}, bf16[128,896]{1,0:T(8,128)(2,1)S(1)}, u32[]{:S(2)}) copy-start(bf16[128,896]{1,0:T(8,128)(2,1)S(1)} %get-tuple-element.14) | copy-start | bytes 688132
  170.3 10.7 %slice-start = ((s8[7340032]{0:T(1024)(128)(4,1)}), s8[3145728]{0:T(1024)(128)(4,1)S(1)}, s32[]{:S(2)}) async-start(s8[7340032]{0:T(1024)(128)(4,1)} %bitcast.53), calls=%async_computation.9 | async-start | bytes 6291456
  176.5 4.5 %copy-start.2 = (bf16[128,896]{1,0:T(8,128)(2,1)}, bf16[128,896]{1,0:T(8,128)(2,1)S(1)}, u32[]{:S(2)}) copy-start(bf16[128,896]{1,0:T(8,128)(2,1)S(1)} %get-tuple-element.12) | copy-start | bytes 688132
  176.5 4.5 %slice-start.1 = ((s8[7340032]{0:T(1024)(128)(4,1)}), s8[4194304]{0:T(1024)(128)(4,1)S(1)}, s32[]{:S(2)}) async-start(s8[7340032]{0:T(1024)(128)(4,1)} %bitcast.53), calls=%async_computation.10 | async-start | bytes 8388608
  184.2 6.1 %copy-start.4 = (bf16[128,896]{1,0:T(8,128)(2,1)S(1)}, bf16[128,896]{1,0:T(8,128)(2,1)}, u32[]{:S(2)}) copy-start(bf16[128,896]{1,0:T(8,128)(2,1)} %copy-done.3) | copy-start | bytes 688132
  246.1 8.5 %all-to-all-start.4 = ((bf16[4,4,4096]{2,1,0:T(4,128)(2,1)}), bf16[4,4,4096]{2,1,0:T(4,128)(2,1)S(1)}, u32[]{:S(2)}, u32[]{:S(2)}) async-start(bf16[4,4,4096]{2,1,0:T(4,128)(2,1)} %reshape.79), calls=%async_computation.5 | async-start | bytes 262144 | tf_op jit(solution)/shard_map/all_to_all | solution.py:94
Sparse Core Ops, SparseCore 0:
  17.6 41.0 all-gather.5
  60.8 39.1 all-gather.3
  183.5 60.9 reduce-scatter.1
where the time goes:
time: 263 us; the launch traced here: 262 us
  waiting for transfers between devices  110 us (42%)
  blocking collectives  74.2 us (28%)
  matrix products  44.8 us (17%)
  between operations  14.6 us (6%)
  local copies, waits for them, and re-layouts  11.1 us (4%)
  other arithmetic  4.09 us (2%)
  starting transfers between devices  3.44 us (1%)
    reduce_scatter x1, waiting for transfers between devices, on_device(): lax.psum_scatter((jnp.dot(gate_pre_grad, gate_weight, preferred_element_t...  49 us
    all_gather x1, waiting for transfers between devices, on_device(): lax.all_gather(owned_grads[0], 'replica', axis=0, tiled=True)  31 us
    all_gather x1, waiting for transfers between devices, on_device(): column_inputs = lax.all_gather(owned_inputs, 'replica', axis=0, tiled=True)  29.6 us
    all_gather x1, blocking collectives, on_device(): lax.all_gather(owned_grads[1].astype(jnp.bfloat16), 'replica', axis=0, ti...  26.3 us
    unnamed x1, blocking collectives  19.2 us
    all_to_all x1, blocking collectives, on_device(): lax.all_to_all(send_inputs, 'expert', split_axis=0, concat_axis=0, tiled=...  8.74 us
    all_to_all x1, blocking collectives, on_device(): lax.all_to_all(send_grads, 'expert', split_axis=0, concat_axis=0, tiled=T...  7.64 us
    all_to_all x1, blocking collectives, on_device(): lax.all_to_all(summed_products.reshape(owners, capacity), 'expert', split...  6.31 us
  transfers between devices with their start and end apart: 4, of which 3 were waited for; matrix products, arithmetic and copies ran while one was open for 12% of the time, Pallas kernels for 0%

commit v1 on v0

v1 whole, which is shorter than its diff:
```python
import functools

import jax
import jax.numpy as jnp
from jax import lax
from jax.experimental import pallas as pl
from jax.experimental.pallas import tpu as pltpu
from jax.sharding import PartitionSpec as P

MESH = pl.DeviceIdType.MESH
PAD = 8
CORES = 2
CHUNKS = 4
VMEM_LIMIT = 67043328
F32 = jnp.float32
BF16 = jnp.bfloat16
NT = (((1,), (1,)), ((), ()))


def split_replica(count):
    fast = max(n for n in range(1, count + 1) if count % n == 0 and n * n <= count)
    return count // fast, fast


def exchange_kernel(
    owners, slow, fast, capacity, rows, fan_out,
    tok_ref, grad_ref, meta_ref, wg_hbm, wu_hbm, wd_hbm,
    x_ref, scaled_ref, hid_t_ref, gpg_t_ref, upg_t_ref, gate_grad_ref, input_grad_ref,
    wg, wu, wd, tok_all, grad_all, meta_all, gate_pre, up_pre, out_dot, hidden, gpg, upg,
    ypart, yrecv, zpart, zrecv, epart, erecv, vals, vy, vz, ve,
    w_sem, g_send, g_recv, y_send, y_recv, z_send, z_recv, e_send, e_recv, v_send, v_recv,
):
    replicas = slow * fast
    chips = owners // CORES
    me_e, me_r = lax.axis_index("expert"), lax.axis_index("replica")
    me_s, me_f = me_r // fast, me_r % fast
    me_x, me_k = me_e // CORES, me_e % CORES
    width = x_ref.shape[1]
    slots = x_ref.shape[0]
    chunk = width // CHUNKS

    sizes = {"z": slow, "y": fast, "x": chips, "k": CORES}
    place = {"z": me_s, "y": me_f, "x": me_x, "k": me_k}

    def device(pos):
        return (pos["x"] * CORES + pos["k"], pos["z"] * fast + pos["y"])

    def moved(dim, step):
        pos = dict(place)
        pos[dim] = lax.rem(place[dim] + step + sizes[dim], sizes[dim])
        return pos

    loads = []
    for i, (src, dst) in enumerate(((wg_hbm, wg), (wu_hbm, wu), (wd_hbm, wd))):
        loads.append(pltpu.make_async_copy(src, dst, w_sem.at[i]))
        loads[-1].start()

    barrier = pltpu.get_barrier_semaphore()
    peers = [device(moved("z", i)) for i in range(1, slow)]
    peers += [device(moved("y", i)) for i in range(1, fast)]
    peers += [(lax.rem(me_e + i, owners), me_r) for i in range(1, owners)]
    for peer in peers:
        pl.semaphore_signal(barrier, inc=1, device_id=peer, device_id_type=MESH)
    pl.semaphore_wait(barrier, len(peers))

    def origin(offset):
        pos = {d: lax.rem(place[d] - offset.get(d, 0) + sizes[d], sizes[d]) for d in place}
        e, r = device(pos)
        return e * replicas + r

    sent = []

    def forward(which, own, everyone, order, offset, last):
        block = origin(offset)
        for dim in order[last + 1:]:
            for step in range(1, sizes[dim]):
                src = own if not offset else everyone.at[block]
                copy = pltpu.make_async_remote_copy(
                    src_ref=src, dst_ref=everyone.at[block],
                    send_sem=g_send.at[which, counts[which]], recv_sem=g_recv.at[which, block],
                    device_id=device(moved(dim, step)), device_id_type=MESH,
                )
                counts[which] += 1
                copy.start()
                sent.append(copy)

    counts = [0, 0, 0]
    streams = (
        (2, meta_ref, meta_all, "zyxk"),
        (0, tok_ref, tok_all, "zyxk"),
        (1, grad_ref, grad_all, "zxyk"),
    )
    for which, own, everyone, order in streams:
        forward(which, own, everyone, order, {}, -1)
    me = me_e * replicas + me_r
    for which, own, everyone, order in streams:
        everyone[me] = own[...]
    held = {0: [{}], 1: [{}], 2: [{}]}
    for level in range(4):
        fresh = {0: [], 1: [], 2: []}
        for position in range(len(held[0]) * (max(sizes.values()) - 1)):
            for which, own, everyone, order in streams:
                dim = order[level]
                steps = sizes[dim] - 1
                if position >= len(held[which]) * steps:
                    continue
                base = held[which][position // steps]
                offset = dict(base)
                offset[dim] = position % steps + 1
                block = origin(offset)
                pltpu.make_async_remote_copy(
                    src_ref=everyone.at[block], dst_ref=everyone.at[block],
                    send_sem=g_send.at[which, 0], recv_sem=g_recv.at[which, block],
                    device_id=device(moved("k", 1)), device_id_type=MESH,
                ).wait_recv()
                forward(which, own, everyone, order, offset, level)
                fresh[which].append(offset)
        for which in held:
            held[which] = held[which] + fresh[which]

    total = tok_all.shape[0] * PAD
    meta_t = jnp.transpose(meta_all[...].reshape(total, meta_all.shape[2]))
    lane = lax.broadcasted_iota(jnp.int32, meta_t.shape, 0)
    slot_row = jnp.sum(jnp.where(lane == me_e, meta_t, 0.0), axis=0, keepdims=True)
    gate_row = jnp.sum(jnp.where(lane == me_e + owners, meta_t, 0.0), axis=0, keepdims=True)
    slot_ids = lax.broadcasted_iota(jnp.int32, (slots, total), 0).astype(F32)
    pick = slot_ids == slot_row
    slot_gate = jnp.sum(jnp.where(pick, gate_row, 0.0), axis=1, keepdims=True)
    chosen = jnp.where(pick, 1.0, 0.0).astype(BF16)

    piece = 512

    def columns(c):
        return pl.ds(pl.multiple_of(c * piece, piece), piece)

    for load in loads:
        load.wait()

    gate_pre[...] = jnp.zeros_like(gate_pre)
    up_pre[...] = jnp.zeros_like(up_pre)
    out_dot[...] = jnp.zeros_like(out_dot)

    @pl.loop(0, width // piece)
    def _(c):
        cols = columns(c)
        toks = tok_all[:, :, cols].reshape(total, piece)
        x = jnp.dot(chosen, toks, preferred_element_type=F32).astype(BF16)
        x_ref[:, cols] = x
        grads = grad_all[:, :, cols].reshape(total, piece)
        routed = jnp.dot(chosen, grads, preferred_element_type=F32)
        scaled_ref[:, cols] = (slot_gate * routed).astype(BF16)
        gate_pre[...] += lax.dot_general(x, wg[:, cols], NT, preferred_element_type=F32)
        up_pre[...] += lax.dot_general(x, wu[:, cols], NT, preferred_element_type=F32)
        out_dot[...] += lax.dot_general(
            routed.astype(BF16), wd[:, cols], NT, preferred_element_type=F32
        )

    g, u, v = gate_pre[...], up_pre[...], out_dot[...]
    h = slot_gate * v
    sig = jax.nn.sigmoid(g)
    active = g * sig
    hid = (active * u).astype(BF16)
    hidden[...] = hid
    gpg[...] = (h * u * sig * (1.0 + g * (1.0 - sig))).astype(BF16)
    upg[...] = (h * active).astype(BF16)
    value = jnp.sum(hid.astype(F32) * v, axis=1, keepdims=True)

    def send(src, dst, send_sem, recv_sem, target):
        copy = pltpu.make_async_remote_copy(
            src_ref=src, dst_ref=dst, send_sem=send_sem, recv_sem=recv_sem,
            device_id=target, device_id_type=MESH,
        )
        copy.start()
        sent.append(copy)
        return copy

    y_copies, z_copies, e_copies = [], [], []
    y_rows = slow * owners * capacity
    z_rows = owners * capacity
    for j in range(CHUNKS):
        for q in range(chunk // piece):
            cols = pl.ds(j * chunk + q * piece, piece)
            part = jnp.dot(gpg[...], wg[:, cols], preferred_element_type=F32) + jnp.dot(
                upg[...], wu[:, cols], preferred_element_type=F32
            )
            ypart[j, :, :, pl.ds(q * piece, piece)] = part.astype(BF16).reshape(fast, y_rows, piece)
        y_copies.append([
            send(ypart.at[j, lax.rem(me_f + i, fast)], yrecv.at[j, i - 1],
                 y_send.at[j, i - 1], y_recv.at[j, i - 1], device(moved("y", i)))
            for i in range(1, fast)
        ])

    spread = jnp.transpose(jnp.broadcast_to(value, (slots, 128)))
    vals[0] = spread[:PAD]
    vy_copies = [
        send(vals.at[0], vy.at[i - 1], v_send.at[0, i - 1], v_recv.at[0, i - 1], device(moved("y", i)))
        for i in range(1, fast)
    ]
    hid_t_ref[...] = jnp.transpose(hidden[...])
    gpg_t_ref[...] = jnp.transpose(gpg[...])
    upg_t_ref[...] = jnp.transpose(upg[...])

    for j in range(CHUNKS):
        acc = ypart[j, me_f].astype(F32)
        for i in range(1, fast):
            y_copies[j][i - 1].wait_recv()
            acc += yrecv[j, i - 1].astype(F32)
        zpart[j] = acc.astype(BF16).reshape(slow, z_rows, chunk)
        z_copies.append([
            send(zpart.at[j, lax.rem(me_s + i, slow)], zrecv.at[j, i - 1],
                 z_send.at[j, i - 1], z_recv.at[j, i - 1], device(moved("z", i)))
            for i in range(1, slow)
        ])
        if j == 0:
            acc_v = vals[0]
            for i in range(1, fast):
                vy_copies[i - 1].wait_recv()
                acc_v += vy[i - 1]
            vals[1] = acc_v
            vz_copies = [
                send(vals.at[1], vz.at[i - 1], v_send.at[1, i - 1], v_recv.at[1, i - 1],
                     device(moved("z", i)))
                for i in range(1, slow)
            ]

    for j in range(CHUNKS):
        acc = zpart[j, me_s].astype(F32)
        for i in range(1, slow):
            z_copies[j][i - 1].wait_recv()
            acc += zrecv[j, i - 1].astype(F32)
        for e in range(owners):
            epart[j, e] = acc[e * capacity:(e + 1) * capacity].astype(BF16)
        e_copies.append([
            send(epart.at[j, lax.rem(me_e + i, owners)], erecv.at[j, i - 1],
                 e_send.at[j, i - 1], e_recv.at[j, i - 1], (lax.rem(me_e + i, owners), me_r))
            for i in range(1, owners)
        ])
        if j == 0:
            acc_v = vals[1]
            for i in range(1, slow):
                vz_copies[i - 1].wait_recv()
                acc_v += vz[i - 1]
            vals[2] = acc_v
            ve_copies = [
                send(vals.at[2], ve.at[i - 1], v_send.at[2, i - 1], v_recv.at[2, i - 1],
                     (lax.rem(me_e + i, owners), me_r))
                for i in range(1, owners)
            ]

    meta = meta_ref[...]
    meta_lane = lax.broadcasted_iota(jnp.int32, meta.shape, 1)

    def lane_of(index):
        return jnp.sum(jnp.where(meta_lane == index, meta, 0.0), axis=1, keepdims=True)

    base = ((me_f * slow + me_s) * owners) * capacity
    slot_lane = lax.broadcasted_iota(jnp.int32, (PAD, slots), 1).astype(F32)
    ids = [lane_of(2 * owners + k) for k in range(fan_out)]
    grads_k = [jnp.zeros((PAD, 1), F32) for _ in range(fan_out)]
    spots = []
    for i in range(owners):
        e = lax.rem(me_e - i + owners, owners)
        spot = lane_of(e)
        spots.append((e, spot))
        if i:
            ve_copies[i - 1].wait_recv()
        row = vals[2] if i == 0 else ve[i - 1]
        got = jnp.sum(jnp.where(spot == slot_lane, row, 0.0), axis=1, keepdims=True)
        for k in range(fan_out):
            grads_k[k] += jnp.where(ids[k] == e.astype(F32), got, 0.0)
    for k in range(fan_out):
        gate_grad_ref[:, k:k + 1] = grads_k[k][:rows]

    for j in range(CHUNKS):
        acc = jnp.zeros((PAD, chunk), F32)
        for i in range(owners):
            if i:
                e_copies[j][i - 1].wait_recv()
            block = epart[j, me_e] if i == 0 else erecv[j, i - 1]
            block = block.astype(F32)
            rank = spots[i][1] - (base + me_e * capacity).astype(F32)
            for c in range(capacity):
                acc += jnp.where(rank == c, 1.0, 0.0) * block[c:c + 1]
        input_grad_ref[:, j * chunk:(j + 1) * chunk] = acc[:rows].astype(BF16)

    for copy in sent:
        copy.wait_send()


def grads_kernel(hid_t, gpg_t, upg_t, x, scaled, gg, gu, gd):
    gg[...] = jnp.dot(gpg_t[...], x[...], preferred_element_type=F32).astype(BF16)
    gu[...] = jnp.dot(upg_t[...], x[...], preferred_element_type=F32).astype(BF16)
    gd[...] = jnp.dot(hid_t[...], scaled[...], preferred_element_type=F32).astype(BF16)


def on_device(tokens, out_grad, expert_ids, gates, w_gate, w_up, w_down):
    rows, fan_out = expert_ids.shape
    width = tokens.shape[1]
    owners, replicas = lax.axis_size("expert"), lax.axis_size("replica")
    slow, fast = split_replica(replicas)
    capacity = max(2, 4 * rows * fan_out // (3 * owners))
    devices = owners * replicas
    slots = devices * capacity
    units = w_gate.shape[1]
    chips = owners // CORES
    me_e, me_r = lax.axis_index("expert"), lax.axis_index("replica")

    flat = expert_ids.reshape(-1)
    hot = (flat[:, None] == jnp.arange(owners, dtype=jnp.int32)[None, :]).astype(jnp.int32)
    seq = jnp.arange(rows * fan_out, dtype=jnp.int32)
    earlier = (seq[None, :] < seq[:, None]).astype(jnp.int32)
    rank = jnp.sum(earlier[:, :, None] * hot[None, :, :], axis=1)
    base = (((me_r % fast) * slow + me_r // fast) * owners + me_e) * capacity
    spot = jnp.max(jnp.where(hot == 1, rank + base, -1).reshape(rows, fan_out, owners), axis=1)
    gate = jnp.sum(hot.reshape(rows, fan_out, owners).astype(F32) * gates[:, :, None], axis=1)
    meta = jnp.concatenate([spot.astype(F32), gate, expert_ids.astype(F32)], axis=1)
    meta = jnp.pad(meta, ((0, PAD - rows), (0, 128 - meta.shape[1])), constant_values=-1.0)
    pad = ((0, PAD - rows), (0, 0))
    chunk = width // CHUNKS
    vm = pltpu.VMEM
    dma = pltpu.SemaphoreType.DMA
    sh = jax.ShapeDtypeStruct
    vspec = pl.BlockSpec(memory_space=pltpu.VMEM)
    aspec = pl.BlockSpec(memory_space=pl.ANY)
    x, scaled, hid_t, gpg_t, upg_t, gate_grad, input_grad = pl.pallas_call(
        functools.partial(exchange_kernel, owners, slow, fast, capacity, rows, fan_out),
        out_shape=(
            sh((slots, width), BF16), sh((slots, width), BF16),
            sh((units, slots), BF16), sh((units, slots), BF16), sh((units, slots), BF16),
            sh((rows, fan_out), F32), sh((rows, width), BF16),
        ),
        in_specs=[vspec] * 3 + [aspec] * 3,
        out_specs=(vspec,) * 7,
        scratch_shapes=[
            vm((units, width), BF16), vm((units, width), BF16), vm((units, width), BF16),
            vm((devices, PAD, width), BF16), vm((devices, PAD, width), BF16),
            vm((devices, PAD, 128), F32),
            vm((slots, units), F32), vm((slots, units), F32), vm((slots, units), F32),
            vm((slots, units), BF16), vm((slots, units), BF16), vm((slots, units), BF16),
            vm((CHUNKS, fast, slots // fast, chunk), BF16),
            vm((CHUNKS, fast - 1, slots // fast, chunk), BF16),
            vm((CHUNKS, slow, owners * capacity, chunk), BF16),
            vm((CHUNKS, slow - 1, owners * capacity, chunk), BF16),
            vm((CHUNKS, owners, capacity, chunk), BF16),
            vm((CHUNKS, owners - 1, capacity, chunk), BF16),
            vm((3, PAD, slots), F32), vm((fast - 1, PAD, slots), F32),
            vm((slow - 1, PAD, slots), F32), vm((owners - 1, PAD, slots), F32),
            dma((3,)), dma((3, devices)), dma((3, devices)),
            dma((CHUNKS, fast)), dma((CHUNKS, fast)),
            dma((CHUNKS, slow)), dma((CHUNKS, slow)),
            dma((CHUNKS, owners)), dma((CHUNKS, owners)),
            dma((3, max(owners, slow, fast))), dma((3, max(owners, slow, fast))),
        ],
        compiler_params=pltpu.CompilerParams(
            collective_id=0, has_side_effects=True, vmem_limit_bytes=VMEM_LIMIT
        ),
        name="exchange",
    )(jnp.pad(tokens, pad), jnp.pad(out_grad, pad), meta, w_gate[0], w_up[0], w_down[0])

    block = 512
    whole = lambda a: pl.BlockSpec(a.shape, lambda i: (0, 0))
    cols = lambda n: pl.BlockSpec((n, block), lambda i: (0, i))
    gg, gu, gd = pl.pallas_call(
        grads_kernel,
        grid=(width // block,),
        out_shape=(sh((units, width), BF16),) * 3,
        in_specs=[whole(hid_t), whole(gpg_t), whole(upg_t), cols(slots), cols(slots)],
        out_specs=(cols(units),) * 3,
        compiler_params=pltpu.CompilerParams(vmem_limit_bytes=48 * 1024 * 1024),
        name="weight_grads",
    )(hid_t, gpg_t, upg_t, x, scaled)
    return gate_grad, input_grad, gg[None], gu[None], gd[None]


def solution(mesh):
    tok = P(("expert", "replica"), None)
    weight = P("expert", "replica", None)
    return jax.shard_map(
        on_device,
        mesh=mesh,
        in_specs=(tok,) * 4 + (weight,) * 3,
        out_specs=(tok, tok, weight, weight, weight),
        check_vma=False,
    )
```

time: 263 us -> 94.9 us (0.36)
  waiting for transfers between devices: 110 us -> 0 us
  Pallas kernels: 0 us -> 79.9 us
  blocking collectives: 74.2 us -> 0 us
  matrix products: 44.8 us -> 0 us
  between operations: 14.6 us -> 0.71 us
  starting transfers between devices: 3.44 us -> 0 us
  other arithmetic: 4.09 us -> 1.15 us
    pallas_call x0 -> x2, Pallas kernels: none -> 79.9 us  [the longest x1 70.4 us: on_device(): pl.pallas_call(functools.partial(exchange_kernel, owners, slow, fast, cap...]
    all_gather x2 -> x0, waiting for transfers between devices: 60.6 us -> none  [the longest x1 31 us: on_device(): lax.all_gather(owned_grads[0], 'replica', axis=0, tiled=True)]
    reduce_scatter x1 -> x0, waiting for transfers between devices: 49 us -> none  [on_device(): lax.psum_scatter((jnp.dot(gate_pre_grad, gate_weight, preferred_element_t...]
    dot_general x12 -> x0, matrix products: 44.8 us -> none  [the longest x1 6.16 us: on_device(): lax.dot_general(scaled, down_weight, contract, preferred_element_type=jnp...]
    all_to_all x4 -> x0, blocking collectives: 28.8 us -> none  [the longest x1 8.74 us: on_device(): lax.all_to_all(send_inputs, 'expert', split_axis=0, concat_axis=0, tiled=...]
    all_gather x1 -> x0, blocking collectives: 26.3 us -> none  [on_device(): lax.all_gather(owned_grads[1].astype(jnp.bfloat16), 'replica', axis=0, ti...]
    unnamed x1 -> x0, blocking collectives: 19.2 us -> none
    unnamed x21 -> x14, local copies, waits for them, and re-layouts: 3.54 us -> 9.58 us
  transfers between devices with their start and end apart: 4 -> 0, of which waited for: 3 -> 0; matrix products, arithmetic and copies ran while one was open for 12% -> 0% of each run, Pallas kernels for 0% -> 0%
where the time goes in v1:
time: 94.9 us; the launch traced here: 94.4 us
  Pallas kernels  79.9 us (84%)
  local copies, waits for them, and re-layouts  12.6 us (13%)
  other arithmetic  1.15 us (1%)
    pallas_call x1, Pallas kernels, on_device(): pl.pallas_call(functools.partial(exchange_kernel, owners, slow, fast, cap...  70.4 us
    unnamed x14, local copies, waits for them, and re-layouts  9.58 us
    pallas_call x1, Pallas kernels, on_device(): pl.pallas_call(grads_kernel, grid=(width // block,), out_shape=(sh((units...  9.44 us

profile of v1, /device:TPU:0, one launch (start us, length us, event | category | flops | bytes accessed | tf_op | source)
XLA Modules:
  0.0 94.4 jit_solution(12003164241059651825)
XLA Ops:
  0.7 0.8 copy.22
  1.4 0.1 eq.41
  1.5 0.8 copy.24
  2.3 0.1 multiply_reduce_fusion.1
  2.4 0.3 multiply_reduce_fusion
  2.7 0.1 fusion.1
  2.8 0.7 select_maximum_fusion.meta_ref
  3.5 1.5 %pad.11.tok_ref = bf16[8,4096]{1,0:T(8,128)(2,1)} pad(bf16[6,4096]{1,0:T(8,128)(2,1)} %param.7, bf16[]{:T(256)} %constant.34.clone.1), padding=0_2x0_0 | pad | bytes 114690 | tf_op jit(solution)/shard_map/jit(_pad)/pad | solution.py:358
  5.0 1.5 %pad.12.grad_ref = bf16[8,4096]{1,0:T(8,128)(2,1)} pad(bf16[6,4096]{1,0:T(8,128)(2,1)} %param.8, bf16[]{:T(256)} %constant.34.clone.1), padding=0_2x0_0 | pad | bytes 114690 | tf_op jit(solution)/shard_map/jit(_pad)/pad | solution.py:358
  6.4 70.4 %exchange.1 = (bf16[128,4096]{1,0:T(8,128)(2,1)}, bf16[128,4096]{1,0:T(8,128)(2,1)}, bf16[896,128]{1,0:T(8,128)(2,1)}, bf16[896,128]{1,0:T(8,128)(2,1)}, bf16[89...) custom-call(bf16[8,4096]{1,0:T(8,128)(2,1)} %pad.11.tok_ref, bf16[8,4096]{1,0:T(8,128)(2,1)} %pad.12.grad_ref, ...), custom_call_target="tpu_custom_call" | custom-call | tf_op jit(solution)/shard_map/exchange/pallas_call | solution.py:325
  76.9 1.3 %copy.26 = f32[6,2]{0,1:T(2,128)} copy(f32[6,2]{1,0:T(8,128)} %get-tuple-element.35) | data formatting | bytes 96
  78.2 0.0 copy-start
  78.2 1.2 %copy-done = bf16[128,4096]{1,0:T(8,128)(2,1)S(1)} copy-done((bf16[128,4096]{1,0:T(8,128)(2,1)S(1)}, bf16[128,4096]{1,0:T(8,128)(2,1)}, u32[]{:S(2)}) %copy-start) | copy-done | bytes 1048600
  79.4 0.0 copy-start.1
  79.4 1.2 %copy-done.1 = bf16[128,4096]{1,0:T(8,128)(2,1)S(1)} copy-done((bf16[128,4096]{1,0:T(8,128)(2,1)S(1)}, bf16[128,4096]{1,0:T(8,128)(2,1)}, u32[]{:S(2)}) %copy-start.1) | copy-done | bytes 1048600
  80.6 0.0 copy-start.2
  80.6 0.9 copy-done.2
  81.6 0.0 copy-start.3
  81.6 0.9 copy-done.3
  82.5 0.0 copy-start.4
  82.5 0.9 copy-done.4
  83.5 9.4 %weight_grads.1 = (bf16[896,4096]{1,0:T(8,128)(2,1)}, bf16[896,4096]{1,0:T(8,128)(2,1)}, bf16[896,4096]{1,0:T(8,128)(2,1)}) custom-call(bf16[896,128]{1,0:T(8,128)(2,1)S(1)} %copy-done.2, bf16[896,128]{1,0:T(8,128)(2,1)S(1)} %copy-done.3, bf16[896,128]{1,0:T(8,128)(2,1)S(1)} %copy-done.4, bf16[128,4096]{1,0:T(8,128)(2,1)S(1)} %copy-done, ...), custom_call_target="tpu_custom_call" | custom-call | tf_op jit(solution)/shard_map/weight_grads/pallas_call | solution.py:363
  92.9 1.5 %copy.28 = bf16[6,4096]{1,0:T(8,128)(2,1)} copy(bf16[6,4096]{1,0:T(8,128)(2,1)} %get-tuple-element.46) | data formatting | bytes 98304
  (6 shorter events, 0.0 us)
Async XLA Ops:
  78.2 1.2 %copy-start = (bf16[128,4096]{1,0:T(8,128)(2,1)S(1)}, bf16[128,4096]{1,0:T(8,128)(2,1)}, u32[]{:S(2)}) copy-start(bf16[128,4096]{1,0:T(8,128)(2,1)} %get-tuple-element.20.x) | copy-start | bytes 3145732
  79.4 1.2 %copy-start.1 = (bf16[128,4096]{1,0:T(8,128)(2,1)S(1)}, bf16[128,4096]{1,0:T(8,128)(2,1)}, u32[]{:S(2)}) copy-start(bf16[128,4096]{1,0:T(8,128)(2,1)} %get-tuple-element.21.scaled) | copy-start | bytes 3145732
  80.6 0.9 copy-start.2
  81.6 0.9 copy-start.3
  82.5 0.9 copy-start.4

commit v2 on v1

--- a/solution.py
+++ b/solution.py
@@ -177,6 +177,18 @@
     y_copies, z_copies, e_copies = [], [], []
     y_rows = slow * owners * capacity
     z_rows = owners * capacity
+    def pass_on(j):
+        acc = ypart[j, me_f].astype(F32)
+        for i in range(1, fast):
+            y_copies[j][i - 1].wait_recv()
+            acc += yrecv[j, i - 1].astype(F32)
+        zpart[j] = acc.astype(BF16).reshape(slow, z_rows, chunk)
+        z_copies.append([
+            send(zpart.at[j, lax.rem(me_s + i, slow)], zrecv.at[j, i - 1],
+                 z_send.at[j, i - 1], z_recv.at[j, i - 1], device(moved("z", i)))
+            for i in range(1, slow)
+        ])
+
     for j in range(CHUNKS):
         for q in range(chunk // piece):
             cols = pl.ds(j * chunk + q * piece, piece)
@@ -189,6 +201,8 @@
                  y_send.at[j, i - 1], y_recv.at[j, i - 1], device(moved("y", i)))
             for i in range(1, fast)
         ])
+        if j:
+            pass_on(j - 1)
 
     spread = jnp.transpose(jnp.broadcast_to(value, (slots, 128)))
     vals[0] = spread[:PAD]
@@ -200,28 +214,17 @@
     gpg_t_ref[...] = jnp.transpose(gpg[...])
     upg_t_ref[...] = jnp.transpose(upg[...])
 
-    for j in range(CHUNKS):
-        acc = ypart[j, me_f].astype(F32)
-        for i in range(1, fast):
-            y_copies[j][i - 1].wait_recv()
-            acc += yrecv[j, i - 1].astype(F32)
-        zpart[j] = acc.astype(BF16).reshape(slow, z_rows, chunk)
-        z_copies.append([
-            send(zpart.at[j, lax.rem(me_s + i, slow)], zrecv.at[j, i - 1],
-                 z_send.at[j, i - 1], z_recv.at[j, i - 1], device(moved("z", i)))
-            for i in range(1, slow)
-        ])
-        if j == 0:
-            acc_v = vals[0]
-            for i in range(1, fast):
-                vy_copies[i - 1].wait_recv()
-                acc_v += vy[i - 1]
-            vals[1] = acc_v
-            vz_copies = [
-                send(vals.at[1], vz.at[i - 1], v_send.at[1, i - 1], v_recv.at[1, i - 1],
-                     device(moved("z", i)))
-                for i in range(1, slow)
-            ]
+    pass_on(CHUNKS - 1)
+    acc_v = vals[0]
+    for i in range(1, fast):
+        vy_copies[i - 1].wait_recv()
+        acc_v += vy[i - 1]
+    vals[1] = acc_v
+    vz_copies = [
+        send(vals.at[1], vz.at[i - 1], v_send.at[1, i - 1], v_recv.at[1, i - 1],
+             device(moved("z", i)))
+        for i in range(1, slow)
+    ]
 
     for j in range(CHUNKS):
         acc = zpart[j, me_s].astype(F32)
@@ -366,7 +369,7 @@
         out_shape=(sh((units, width), BF16),) * 3,
         in_specs=[whole(hid_t), whole(gpg_t), whole(upg_t), cols(slots), cols(slots)],
         out_specs=(cols(units),) * 3,
-        compiler_params=pltpu.CompilerParams(vmem_limit_bytes=48 * 1024 * 1024),
+        compiler_params=pltpu.CompilerParams(vmem_limit_bytes=VMEM_LIMIT),
         name="weight_grads",
     )(hid_t, gpg_t, upg_t, x, scaled)
     return gate_grad, input_grad, gg[None], gu[None], gd[None]

time: 94.9 us -> 87.7 us (0.924)
  local copies, waits for them, and re-layouts: 12.6 us -> 7.37 us
  Pallas kernels: 79.9 us -> 77.9 us
    unnamed x14 -> x4, local copies, waits for them, and re-layouts: 9.58 us -> 4.32 us
    pallas_call x1, Pallas kernels: 70.4 us -> 67.2 us  [on_device(): pl.pallas_call(functools.partial(exchange_kernel, owners, slow, fast, cap...]
    pallas_call x1, Pallas kernels: 9.44 us -> 10.7 us  [on_device(): pl.pallas_call(grads_kernel, grid=(width // block,), out_shape=(sh((units...]
where the time goes in v2:
time: 87.7 us; the launch traced here: 87.2 us
  Pallas kernels  77.9 us (89%)
  local copies, waits for them, and re-layouts  7.37 us (8%)
  other arithmetic  1.15 us (1%)
    pallas_call x1, Pallas kernels, on_device(): pl.pallas_call(functools.partial(exchange_kernel, owners, slow, fast, cap...  67.2 us
    pallas_call x1, Pallas kernels, on_device(): pl.pallas_call(grads_kernel, grid=(width // block,), out_shape=(sh((units...  10.7 us
    unnamed x4, local copies, waits for them, and re-layouts  4.32 us

profile of v2, /device:TPU:0, one launch (start us, length us, event | category | flops | bytes accessed | tf_op | source)
XLA Modules:
  0.0 87.2 jit_solution(18040093451991447586)
XLA Ops:
  0.7 0.8 copy.22
  1.4 0.1 eq.41
  1.5 0.8 copy.24
  2.3 0.1 multiply_reduce_fusion.1
  2.4 0.3 multiply_reduce_fusion
  2.7 0.1 fusion.1
  2.8 0.7 select_maximum_fusion.meta_ref
  3.5 1.5 %pad.11.tok_ref = bf16[8,4096]{1,0:T(8,128)(2,1)} pad(bf16[6,4096]{1,0:T(8,128)(2,1)} %param.7, bf16[]{:T(256)} %constant.34.clone.1), padding=0_2x0_0 | pad | bytes 114690 | tf_op jit(solution)/shard_map/jit(_pad)/pad | solution.py:361
  5.0 1.5 %pad.12.grad_ref = bf16[8,4096]{1,0:T(8,128)(2,1)} pad(bf16[6,4096]{1,0:T(8,128)(2,1)} %param.8, bf16[]{:T(256)} %constant.34.clone.1), padding=0_2x0_0 | pad | bytes 114690 | tf_op jit(solution)/shard_map/jit(_pad)/pad | solution.py:361
  6.4 67.2 %exchange.1 = (bf16[128,4096]{1,0:T(8,128)(2,1)}, bf16[128,4096]{1,0:T(8,128)(2,1)}, bf16[896,128]{1,0:T(8,128)(2,1)}, bf16[896,128]{1,0:T(8,128)(2,1)}, bf16[89...) custom-call(bf16[8,4096]{1,0:T(8,128)(2,1)} %pad.11.tok_ref, bf16[8,4096]{1,0:T(8,128)(2,1)} %pad.12.grad_ref, ...), custom_call_target="tpu_custom_call" | custom-call | tf_op jit(solution)/shard_map/exchange/pallas_call | solution.py:328
  73.6 1.3 %copy.26 = f32[6,2]{0,1:T(2,128)} copy(f32[6,2]{1,0:T(8,128)} %get-tuple-element.35) | data formatting | bytes 96
  75.0 10.7 %weight_grads.1 = (bf16[896,4096]{1,0:T(8,128)(2,1)}, bf16[896,4096]{1,0:T(8,128)(2,1)}, bf16[896,4096]{1,0:T(8,128)(2,1)}) custom-call(bf16[896,128]{1,0:T(8,128)(2,1)} %get-tuple-element.17.hid_t, bf16[896,128]{1,0:T(8,128)(2,1)} %get-tuple-element.18.gpg_t, bf16[896,128]{1,0:T(8,128)(2,1)} %get-tuple-element.19.upg_t, ...), custom_call_target="tpu_custom_call" | custom-call | tf_op jit(solution)/shard_map/weight_grads/pallas_call | solution.py:366
  85.7 1.5 %copy.28 = bf16[6,4096]{1,0:T(8,128)(2,1)} copy(bf16[6,4096]{1,0:T(8,128)(2,1)} %get-tuple-element.46) | data formatting | bytes 98304
  (6 shorter events, 0.0 us)
